TPU v7x, 32 devices: a whole 2x2x4 slice. The times are simulated.
32 devices in a mesh: batch: 8 (over y, x, core), head: 4 (over z).
Axes of the slice: x: 2, y: 2, z: 4, core: 2. Of those that a mesh axis runs over, the one named last changes fastest.
Arguments:
- inputs: bfloat16 [8, 128, 2048], P(None, 'batch', 'head'), parts along dimension 1, may hold values from -6 to 6
- in_weight: bfloat16 [2048, 4, 384], P(None, 'head'), may hold values from -0.125 to 0.125
- gate_weight: bfloat16 [2048, 4], P(None, 'head'), may hold values from -0.125 to 0.125
- gate_bias: float32 [4], P('head'), may hold values from -2 to 3
- norm_gain: float32 [512], P('head'), may hold values from 0.1 to 1.9
- out_weight: bfloat16 [512, 2048], P('head'), may hold values from -0.375 to 0.375
- inv_gram: float32 [128, 4, 128, 128], P('batch', 'head'), parts along dimension 0, may hold values from -17 to 17, as said below
- value_key: float32 [128, 4, 128, 128], P('batch', 'head'), parts along dimension 0, may hold values from -6 to 6
Outputs:
- layer_out: float32 [8, 128, 2048], P(None, 'batch', 'head'), parts along dimension 1
There are 8 independent parts, one for each index of `batch`. A program takes and returns all parts, laid end to end along the dimension named above; an argument that names none is the same for every part. Nothing has to cross between parts.
Inputs may be any that keep to these rules, and one draw needn't show every extreme that they name: `inv_gram`: each [128, 128] matrix is symmetric positive definite.
All inputs are finite; a program needn't handle non-finite values.
Results may differ from a plain program's by a relative error of at most 0.0029.
Values may be sent and summed in bfloat16 or wider, within the bound.
No kernel may reach another device: no remote copies, remote signals or barrier semaphores. Data moves between devices by JAX's collectives and lax.ppermute only.
A program may use at most 64 MiB of HBM per device.

v0:
```python
import jax
import jax.numpy as jnp
from jax import lax
from jax.sharding import PartitionSpec as P


def advance(gram_inv, memory, projected, gate, gate_bias, head_size):
    batch_rows, local_heads = gate.shape
    pieces = projected.reshape(batch_rows, local_heads, 3 * head_size)
    queries = pieces[..., :head_size]
    keys_now = pieces[..., head_size : 2 * head_size]
    values_now = pieces[..., 2 * head_size :]
    forget = 0.8 + 0.2 * jax.nn.sigmoid(gate + gate_bias)
    keys_now = keys_now * lax.rsqrt(jnp.sum(keys_now * keys_now, axis=-1, keepdims=True) + 1e-06)
    queries = queries * lax.rsqrt(jnp.sum(queries * queries, axis=-1, keepdims=True) + 1e-06)
    gram_key = jnp.einsum("bhij,bhj->bhi", gram_inv, keys_now, precision=lax.Precision.HIGHEST)
    denominator = forget + jnp.sum(keys_now * gram_key, axis=-1)
    gram_inv = (
        gram_inv - gram_key[..., :, None] * gram_key[..., None, :] / denominator[..., None, None]
    ) / forget[..., None, None]
    memory = forget[..., None, None] * memory + values_now[..., :, None] * keys_now[..., None, :]
    gram_query = jnp.einsum("bhij,bhj->bhi", gram_inv, queries, precision=lax.Precision.HIGHEST)
    readout = jnp.einsum("bhij,bhj->bhi", memory, gram_query, precision=lax.Precision.HIGHEST)
    return (gram_inv, memory, readout.reshape(batch_rows, local_heads * head_size))


def local(inputs, in_weight, gate_weight, gate_bias, norm_gain, out_weight, inv_gram, value_key):
    step_count, batch_rows, _ = inputs.shape
    d_model = in_weight.shape[0]
    local_heads = in_weight.shape[1]
    head_size = in_weight.shape[2] // 3
    total_width = local_heads * head_size * lax.axis_size("head")
    weight_flat = in_weight.reshape(d_model, local_heads * 3 * head_size)
    gram_inv = inv_gram
    memory = value_key
    readouts = []
    for position in range(step_count):
        rows = lax.all_gather(inputs[position], "head", axis=1, tiled=True)
        projected = jnp.dot(rows, weight_flat, preferred_element_type=jnp.float32)
        gate = jnp.dot(rows, gate_weight, preferred_element_type=jnp.float32)
        gram_inv, memory, readout = advance(gram_inv, memory, projected, gate, gate_bias, head_size)
        readouts.append(readout)
    readout_all = jnp.stack(readouts, axis=0)
    squares = lax.psum(jnp.sum(readout_all * readout_all, axis=-1), "head")
    hidden = (
        norm_gain * readout_all * lax.rsqrt(squares / total_width + 1e-06)[:, :, None]
    ).astype(jnp.bfloat16)
    partial_out = jnp.dot(
        hidden.reshape(step_count * batch_rows, -1), out_weight, preferred_element_type=jnp.float32
    )
    partial_out = partial_out.reshape(step_count, batch_rows, d_model)
    return lax.psum_scatter(partial_out, "head", scatter_dimension=2, tiled=True)


def solution(mesh):
    in_specs = (
        P(None, "batch", "head"),
        P(None, "head", None),
        P(None, "head"),
        P("head"),
        P("head"),
        P("head", None),
        P("batch", "head", None, None),
        P("batch", "head", None, None),
    )
    out_specs = P(None, "batch", "head")
    return jax.shard_map(local, mesh=mesh, in_specs=in_specs, out_specs=out_specs, check_vma=False)
```

profile of v0, /device:TPU:0, one launch (start us, length us, event | category | flops | bytes accessed | tf_op | source)
XLA Modules:
  0.0 223.0 jit_solution(10314637504935739932)
XLA Ops:
  7.5 14.9 %all-gather = bf16[1,16,2048]{2,1,0:T(8,128)(2,1)S(1)} all-gather(bf16[1,16,512]{2,1,0:T(8,128)(2,1)S(1)} %get-tuple-element.27), channel_id=2, replica_groups=mesh['batch'=8,'head'=4] {'head'}, dimensions={2}, use_global_device_ids=true | all-gather | bytes 81920 | tf_op jit(solution)/shard_map/all_gather | solution.py:38
  23.0 1.7 fusion.132
  27.8 1.9 fusion.134
  29.7 13.3 %all-gather.1 = bf16[1,16,2048]{2,1,0:T(8,128)(2,1)S(1)} all-gather(bf16[1,16,512]{2,1,0:T(8,128)(2,1)S(1)} %get-tuple-element.26), channel_id=3, replica_groups=mesh['batch'=8,'head'=4] {'head'}, dimensions={2}, use_global_device_ids=true | all-gather | bytes 81920 | tf_op jit(solution)/shard_map/all_gather | solution.py:38
  43.4 13.2 %all-gather.3 = bf16[1,16,2048]{2,1,0:T(8,128)(2,1)S(1)} all-gather(bf16[1,16,512]{2,1,0:T(8,128)(2,1)S(1)} %get-tuple-element.24), channel_id=5, replica_groups=mesh['batch'=8,'head'=4] {'head'}, dimensions={2}, use_global_device_ids=true | all-gather | bytes 81920 | tf_op jit(solution)/shard_map/all_gather | solution.py:38
  57.2 13.4 %all-gather.2 = bf16[1,16,2048]{2,1,0:T(8,128)(2,1)S(1)} all-gather(bf16[1,16,512]{2,1,0:T(8,128)(2,1)S(1)} %get-tuple-element.25), channel_id=4, replica_groups=mesh['batch'=8,'head'=4] {'head'}, dimensions={2}, use_global_device_ids=true | all-gather | bytes 81920 | tf_op jit(solution)/shard_map/all_gather | solution.py:38
  73.4 2.2 multiply_add_fusion.3
  77.4 2.1 fusion.127
  79.5 1.7 fusion.124
  83.5 2.6 %fusion.122 = f32[16,1,128]{2,1,0:T(1,128)S(1)} fusion(f32[16,128,1]{1,2,0:T(1,128)S(1)} %convolution_bitcast_fusion.5, f32[16,128]{1,0:T(8,128)S(1)} %bitcast.573, f32[16,128]{1,0:T(8,128)S(1)} %get-tuple-element.44, f32[16]{0:T(128)S(1)} %fusion.81, f32[16,1,128,128]{3,2,1,0:T(8,128)S(1)} %copy-done.2, f32[16,128]{1,0:T(8,128)S(1)} %bitcast.568, ...), kind=kOutput, calls=%fused_computation.122 | convolution fusion | flops 5505024 | bytes 1114304 | tf_op jit(solution)/shard_map/bhij,bhj->bhi/dot_general | solution.py:23
  86.1 1.7 fusion.119
  88.0 13.5 %all-gather.4 = bf16[1,16,2048]{2,1,0:T(8,128)(2,1)S(1)} all-gather(bf16[1,16,512]{2,1,0:T(8,128)(2,1)S(1)} %get-tuple-element.23), channel_id=6, replica_groups=mesh['batch'=8,'head'=4] {'head'}, dimensions={2}, use_global_device_ids=true | all-gather | bytes 81920 | tf_op jit(solution)/shard_map/all_gather | solution.py:38
  106.4 13.1 %all-gather.5 = bf16[1,16,2048]{2,1,0:T(8,128)(2,1)S(1)} all-gather(bf16[1,16,512]{2,1,0:T(8,128)(2,1)S(1)} %get-tuple-element.22), channel_id=7, replica_groups=mesh['batch'=8,'head'=4] {'head'}, dimensions={2}, use_global_device_ids=true | all-gather | bytes 81920 | tf_op jit(solution)/shard_map/all_gather | solution.py:38
  125.0 13.1 %all-gather.6 = bf16[1,16,2048]{2,1,0:T(8,128)(2,1)S(1)} all-gather(bf16[1,16,512]{2,1,0:T(8,128)(2,1)S(1)} %get-tuple-element.28), channel_id=8, replica_groups=mesh['batch'=8,'head'=4] {'head'}, dimensions={2}, use_global_device_ids=true | all-gather | bytes 81920 | tf_op jit(solution)/shard_map/all_gather | solution.py:38
  144.1 13.5 %all-gather.7 = bf16[1,16,2048]{2,1,0:T(8,128)(2,1)S(1)} all-gather(bf16[1,16,512]{2,1,0:T(8,128)(2,1)S(1)} %get-tuple-element.21), channel_id=9, replica_groups=mesh['batch'=8,'head'=4] {'head'}, dimensions={2}, use_global_device_ids=true | all-gather | bytes 81920 | tf_op jit(solution)/shard_map/all_gather | solution.py:38
  158.1 2.0 subtract_divide_fusion
  161.9 1.7 fusion.99
  165.5 1.9 fusion.112
  167.4 2.1 fusion.107
  169.5 2.6 %fusion.102 = f32[16,1,128]{2,1,0:T(1,128)S(1)} fusion(f32[16,128,1]{1,2,0:T(1,128)S(1)} %convolution_bitcast_fusion.1, f32[16,128]{1,0:T(8,128)S(1)} %bitcast.579, f32[16,128]{1,0:T(8,128)S(1)} %get-tuple-element.32, f32[16]{0:T(128)S(1)} %get-tuple-element.64, f32[16,1,128,128]{3,2,1,0:T(8,128)S(1)} %get-tuple-element.53, f32[16,128]{1,0:T(8,128)S(1)} %bitcast.576, ...), kind=kOutput, calls=%fused_computation.102 | convolution fusion | flops 5505024 | bytes 1114304 | tf_op jit(solution)/shard_map/bhij,bhj->bhi/dot_general | solution.py:23
  172.3 1.9 convolution_bitcast_fusion
  174.2 3.3 %fusion.97 = f32[16,1,128]{2,1,0:T(1,128)S(1)} fusion(f32[16,128,1]{1,2,0:T(1,128)S(1)} %convolution_bitcast_fusion, f32[16,128]{1,0:T(8,128)S(1)} %bitcast.582, f32[16,128]{1,0:T(8,128)S(1)} %get-tuple-element.29, f32[16]{0:T(128)S(1)} %get-tuple-element.66, f32[16,128]{1,0:T(8,128)S(1)} %bitcast.580, f32[16,128]{1,0:T(8,128)S(1)} %get-tuple-element.32, ...), kind=kOutput, calls=%fused_computation.97 | convolution fusion | flops 6291456 | bytes 1130752 | tf_op jit(solution)/shard_map/bhij,bhj->bhi/dot_general | solution.py:23
  177.6 11.6 %psum.7 = f32[8,16]{1,0:T(8,128)S(1)} all-reduce(f32[8,16]{1,0:T(8,128)S(1)} %multiply_reduce_fusion), channel_id=1, replica_groups=mesh['batch'=8,'head'=4] {'head'}, use_global_device_ids=true, to_apply=%region_25.0 | all-reduce | flops 128 | bytes 1024 | tf_op jit(solution)/shard_map/psum | solution.py:44
  190.5 25.6 %reduce-scatter.2.cloned.1.call-done = f32[8,16,512]{2,1,0:T(8,128)} async-done(((f32[8,16,2048]{2,1,0:T(8,128)}), f32[8,16,512]{2,1,0:T(8,128)}) %reduce-scatter.2.cloned.1.call-update) | async-done | bytes 262160 | tf_op jit(solution)/shard_map/reduce_scatter | solution.py:52
  (93 shorter events, 33.9 us)
Async XLA Ops:
  6.5 15.9 %copy-start = (bf16[2048,1,384]{2,0,1:T(8,128)(2,1)S(1)}, bf16[2048,1,384]{2,0,1:T(8,128)(2,1)}, u32[]{:S(2)}) copy-start(bf16[2048,1,384]{2,0,1:T(8,128)(2,1)} %param.9) | copy-start | bytes 4718596
  6.5 16.4 %copy-start.1 = (f32[16,1,128,128]{3,2,1,0:T(8,128)S(1)}, f32[16,1,128,128]{3,2,1,0:T(8,128)}, u32[]{:S(2)}) copy-start(f32[16,1,128,128]{3,2,1,0:T(8,128)} %param.14) | copy-start | bytes 3145732
  6.5 19.0 %copy-start.5 = (bf16[2048,1]{0,1:T(2,128)(2,1)S(1)}, bf16[2048,1]{0,1:T(2,128)(2,1)}, u32[]{:S(2)}) copy-start(bf16[2048,1]{0,1:T(2,128)(2,1)} %param.10) | copy-start | bytes 12292
  6.5 209.6 %reduce-scatter.2.cloned.1.call-start = ((), (), s32[]{:S(2)}) async-start(), calls=%async_computation.1 | async-start | bytes 1310720 | tf_op jit(solution)/shard_map/reduce_scatter | solution.py:52
  25.7 2.1 copy-start.2
  174.2 15.0 %copy-start.3 = (bf16[128,2048]{1,0:T(8,128)(2,1)S(1)}, bf16[128,2048]{1,0:T(8,128)(2,1)}, u32[]{:S(2)}) copy-start(bf16[128,2048]{1,0:T(8,128)(2,1)} %param.13) | copy-start | bytes 1572868
  174.2 15.0 %copy-start.4 = (f32[128]{0:T(128)S(1)}, f32[128]{0:T(128)}, u32[]{:S(2)}) copy-start(f32[128]{0:T(128)} %param.12) | copy-start | bytes 1540
Sparse Core Ops, SparseCore 0:
  190.6 25.4 reduce-scatter.1
where the time goes:
time: 223 us
  blocking collectives  120 us (54%)
  matrix products  50.9 us (23%)
  waiting for transfers between devices  25.7 us (12%)
  between operations  14.4 us (6%)
  other arithmetic  11.4 us (5%)
    all_gather x8, blocking collectives, local(): rows = lax.all_gather(inputs[position], 'head', axis=1, tiled=True)  108 us
    reduce_scatter x1, waiting for transfers between devices, local(): lax.psum_scatter(partial_out, 'head', scatter_dimension=2, tiled=True)  25.6 us
    dot_general x8, matrix products, advance(): jnp.einsum('bhij,bhj->bhi', memory, gram_query, precision=lax.Precision.H...  18.2 us
    dot_general x8, matrix products, advance(): jnp.einsum('bhij,bhj->bhi', gram_inv, queries, precision=lax.Precision.HI...  13.9 us
    dot_general x8, matrix products, advance(): jnp.einsum('bhij,bhj->bhi', gram_inv, keys_now, precision=lax.Precision.H...  13.9 us
    psum x1, blocking collectives, local(): squares = lax.psum(jnp.sum(readout_all * readout_all, axis=-1), 'head')  11.6 us
    div x6, other arithmetic, advance(): (gram_inv - gram_key[..., :, None] * gram_key[..., None, :] / denominator...  6.41 us
  transfers between devices with their start and end apart: 1, of which 1 were waited for; matrix products, arithmetic and copies ran while one was open for 0% of the time, Pallas kernels for 0%

commit v1 on v0

--- a/solution.py
+++ b/solution.py
@@ -35,7 +35,14 @@
     memory = value_key
     readouts = []
     for position in range(step_count):
-        rows = lax.all_gather(inputs[position], "head", axis=1, tiled=True)
+        x = inputs[position]
+        ways, here, step = (lax.axis_size("head"), lax.axis_index("head"), x.shape[1])
+        dims = [n * ways if d == 1 else n for d, n in enumerate(x.shape)]
+        full = lax.dynamic_update_slice_in_dim(jnp.zeros(dims, x.dtype), x, here * step, axis=1)
+        for far in range(1, ways):
+            x = lax.ppermute(x, "head", [(d, (d + 1) % ways) for d in range(ways)])
+            full = lax.dynamic_update_slice_in_dim(full, x, (here - far) % ways * step, axis=1)
+        rows = full
         projected = jnp.dot(rows, weight_flat, preferred_element_type=jnp.float32)
         gate = jnp.dot(rows, gate_weight, preferred_element_type=jnp.float32)
         gram_inv, memory, readout = advance(gram_inv, memory, projected, gate, gate_bias, head_size)

time: 223 us -> 155 us (0.70)
  blocking collectives: 120 us -> 11.6 us
  starting transfers between devices: 0.01 us -> 31.2 us
  local copies, waits for them, and re-layouts: 1.04 us -> 7.18 us
    all_gather x8 -> x0, blocking collectives: 108 us -> none  [local(): rows = lax.all_gather(inputs[position], 'head', axis=1, tiled=True)]
    ppermute x0 -> x24, starting transfers between devices: none -> 31.2 us  [local(): x = lax.ppermute(x, 'head', [(d, (d + 1) % ways) for d in range(ways)])]
    dynamic_update_slice x0 -> x29, local copies, waits for them, and re-layouts: none -> 5.89 us  [the longest x8 5.81 us: local(): lax.dynamic_update_slice_in_dim(jnp.zeros(dims, x.dtype), x, here * step,...]
  transfers between devices with their start and end apart: 1 -> 25, of which waited for: 1 -> 2; matrix products, arithmetic and copies ran while one was open for 0% -> 27% of each run, Pallas kernels for 0% -> 0%
where the time goes in v1:
time: 155 us; the launch traced here: 154 us
  matrix products  51.2 us (33%)
  starting transfers between devices  31.2 us (20%)
  waiting for transfers between devices  26.2 us (17%)
  between operations  14.6 us (9%)
  other arithmetic  11.7 us (8%)
  blocking collectives  11.6 us (7%)
  local copies, waits for them, and re-layouts  7.18 us (5%)
    ppermute x24, starting transfers between devices, local(): x = lax.ppermute(x, 'head', [(d, (d + 1) % ways) for d in range(ways)])  31.2 us
    reduce_scatter x1, waiting for transfers between devices, local(): lax.psum_scatter(partial_out, 'head', scatter_dimension=2, tiled=True)  25.6 us
    dot_general x8, matrix products, advance(): jnp.einsum('bhij,bhj->bhi', memory, gram_query, precision=lax.Precision.H...  18.4 us
    dot_general x8, matrix products, advance(): jnp.einsum('bhij,bhj->bhi', gram_inv, queries, precision=lax.Precision.HI...  13.9 us
    dot_general x8, matrix products, advance(): jnp.einsum('bhij,bhj->bhi', gram_inv, keys_now, precision=lax.Precision.H...  13.9 us
    psum x1, blocking collectives, local(): squares = lax.psum(jnp.sum(readout_all * readout_all, axis=-1), 'head')  11.6 us
    div x6, other arithmetic, advance(): (gram_inv - gram_key[..., :, None] * gram_key[..., None, :] / denominator...  6.64 us
    dynamic_update_slice x8, local copies, waits for them, and re-layouts, local(): lax.dynamic_update_slice_in_dim(jnp.zeros(dims, x.dtype), x, here * step,...  5.81 us
  transfers between devices with their start and end apart: 25, of which 2 were waited for; matrix products, arithmetic and copies ran while one was open for 27% of the time, Pallas kernels for 0%

profile of v1, /device:TPU:0, one launch (start us, length us, event | category | flops | bytes accessed | tf_op | source)
XLA Modules:
  0.0 153.7 jit_solution(891321028439918103)
XLA Ops:
  7.5 3.1 %collective-permute-start.3 = (bf16[16,512]{1,0:T(8,128)(2,1)S(1)}, bf16[16,512]{1,0:T(8,128)(2,1)S(1)}, u32[]{:S(2)}, u32[]{:S(2)}) collective-permute-start(bf16[16,512]{1,0:T(8,128)(2,1)S(1)} %get-tuple-element.26), channel_id=1, source_target_pairs={{0,1},{1,2},{2,3},{3,0},{4,5},{5,6},{6,7},{7,4},{8,9},{9,10},{10,1... | collective-permute-start | bytes 49160 | tf_op jit(solution)/shard_map/ppermute | solution.py:43
  13.8 1.7 %collective-permute-start.15 = (bf16[16,512]{1,0:T(8,128)(2,1)S(1)}, bf16[16,512]{1,0:T(8,128)(2,1)S(1)}, u32[]{:S(2)}, u32[]{:S(2)}) collective-permute-start(bf16[16,512]{1,0:T(8,128)(2,1)S(1)} %get-tuple-element.22), channel_id=1, source_target_pairs={{0,1},{1,2},{2,3},{3,0},{4,5},{5,6},{6,7},{7,4},{8,9},{9,10},{10,1... | collective-permute-start | bytes 49160 | tf_op jit(solution)/shard_map/ppermute | solution.py:43
  46.5 1.7 %fusion.132 = f32[16,1,128]{2,1,0:T(1,128)S(1)} fusion(f32[16,128,1]{1,2,0:T(1,128)S(1)} %bitcast.547, f32[16,1,128,128]{3,2,1,0:T(8,128)S(1)} %copy-done.1), kind=kOutput, calls=%fused_computation.132 | convolution fusion | flops 3145728 | bytes 1064960 | tf_op jit(solution)/shard_map/bhij,bhj->bhi/dot_general | solution.py:16
  52.5 1.7 %fusion.129 = f32[16,1,128]{2,1,0:T(1,128)S(1)} fusion(f32[16,128,1]{1,2,0:T(1,128)S(1)} %bitcast.561, f32[16,1,128,128]{3,2,1,0:T(8,128)S(1)} %subtract_divide_fusion.6), kind=kOutput, calls=%fused_computation.129 | convolution fusion | flops 3145728 | bytes 1064960 | tf_op jit(solution)/shard_map/bhij,bhj->bhi/dot_general | solution.py:16
  54.7 1.8 %fusion.134 = f32[16,1,128]{2,1,0:T(1,128)S(1)} fusion(f32[16,128,1]{1,2,0:T(1,128)S(1)} %convolution_bitcast_fusion.7, f32[16,1,128,128]{3,2,1,0:T(8,128)S(1)} %copy-done.2, f32[16,128]{1,0:T(8,128)S(1)} %bitcast.548, f32[16,128]{1,0:T(8,128)S(1)} %get-tuple-element.50, f32[16]{0:T(128)S(1)} %get-tuple-element.56), kind=kOutput, calls=%fused_computation.134 | convolution fusion | flops 3932160 | bytes 1081408 | tf_op jit(solution)/shard_map/bhij,bhj->bhi/dot_general | solution.py:23
  56.6 2.4 %multiply_add_fusion.3 = (f32[16,1,128,128]{3,2,1,0:T(8,128)S(1)}, f32[16,1,128,128]{3,2,1,0:T(8,128)S(1)}) fusion(f32[16,128]{1,0:T(8,128)S(1)} %bitcast.565, f32[16,128]{1,0:T(8,128)S(1)} %get-tuple-element.41, f32[16]{0:T(128)S(1)} %fusion.74, f32[16,128]{1,0:T(8,128)S(1)} %bitcast.567, f32[16,128]{1,0:T(8,128)S(1)} %get-tuple-element.44, ...), kind=kLoop, calls=%fused_computation.150 | loop fusion | flops 5242880 | bytes 4276608 | tf_op jit(solution)/shard_map/add | solution.py:21
  60.6 2.1 %fusion.127 = f32[16,1,128]{2,1,0:T(1,128)S(1)} fusion(f32[16,128,1]{1,2,0:T(1,128)S(1)} %convolution_bitcast_fusion.6, f32[16,1,128,128]{3,2,1,0:T(8,128)S(1)} %copy-done.2, f32[16,128]{1,0:T(8,128)S(1)} %bitcast.563, f32[16,128]{1,0:T(8,128)S(1)} %get-tuple-element.47, f32[16]{0:T(128)S(1)} %get-tuple-element.58, f32[16,128]{1,0:T(8,128)S(1)} %bitcast.550, ...), kind=kOutput, calls=%fused_computation.127 | convolution fusion | flops 4718592 | bytes 1097856 | tf_op jit(solution)/shard_map/bhij,bhj->bhi/dot_general | solution.py:23
  62.8 1.7 %fusion.124 = f32[16,1,128]{2,1,0:T(1,128)S(1)} fusion(f32[16,128,1]{1,2,0:T(1,128)S(1)} %bitcast.568, f32[16,1,128,128]{3,2,1,0:T(8,128)S(1)} %get-tuple-element.54), kind=kOutput, calls=%fused_computation.124 | convolution fusion | flops 3145728 | bytes 1064960 | tf_op jit(solution)/shard_map/bhij,bhj->bhi/dot_general | solution.py:16
  65.0 1.7 %convolution_bitcast_fusion.5 = f32[16,128,1]{1,2,0:T(1,128)S(1)} fusion(f32[16,128,1]{1,2,0:T(1,128)S(1)} %bitcast.584, f32[16,1,128,128]{3,2,1,0:T(8,128)S(1)} %subtract_divide_fusion.4), kind=kOutput, calls=%fused_computation.29 | convolution fusion | flops 3145728 | bytes 1064960 | tf_op jit(solution)/shard_map/bhij,bhj->bhi/dot_general | solution.py:22
  66.8 2.6 %fusion.122 = f32[16,1,128]{2,1,0:T(1,128)S(1)} fusion(f32[16,128,1]{1,2,0:T(1,128)S(1)} %convolution_bitcast_fusion.5, f32[16,128]{1,0:T(8,128)S(1)} %bitcast.569, f32[16,128]{1,0:T(8,128)S(1)} %get-tuple-element.44, f32[16]{0:T(128)S(1)} %fusion.81, f32[16,1,128,128]{3,2,1,0:T(8,128)S(1)} %copy-done.2, f32[16,128]{1,0:T(8,128)S(1)} %bitcast.564, ...), kind=kOutput, calls=%fused_computation.122 | convolution fusion | flops 5505024 | bytes 1114304 | tf_op jit(solution)/shard_map/bhij,bhj->bhi/dot_general | solution.py:23
  69.4 1.7 %fusion.119 = f32[16,1,128]{2,1,0:T(1,128)S(1)} fusion(f32[16,128,1]{1,2,0:T(1,128)S(1)} %bitcast.566, f32[16,1,128,128]{3,2,1,0:T(8,128)S(1)} %subtract_divide_fusion.4), kind=kOutput, calls=%fused_computation.119 | convolution fusion | flops 3145728 | bytes 1064960 | tf_op jit(solution)/shard_map/bhij,bhj->bhi/dot_general | solution.py:16
  74.3 1.7 %fusion.114 = f32[16,1,128]{2,1,0:T(1,128)S(1)} fusion(f32[16,128,1]{1,2,0:T(1,128)S(1)} %bitcast.556, f32[16,1,128,128]{3,2,1,0:T(8,128)S(1)} %subtract_divide_fusion.3), kind=kOutput, calls=%fused_computation.114 | convolution fusion | flops 3145728 | bytes 1064960 | tf_op jit(solution)/shard_map/bhij,bhj->bhi/dot_general | solution.py:16
  80.1 1.7 %fusion.109 = f32[16,1,128]{2,1,0:T(1,128)S(1)} fusion(f32[16,128,1]{1,2,0:T(1,128)S(1)} %bitcast.570, f32[16,1,128,128]{3,2,1,0:T(8,128)S(1)} %subtract_divide_fusion.2), kind=kOutput, calls=%fused_computation.109 | convolution fusion | flops 3145728 | bytes 1064960 | tf_op jit(solution)/shard_map/bhij,bhj->bhi/dot_general | solution.py:16
  86.0 1.7 %fusion.104 = f32[16,1,128]{2,1,0:T(1,128)S(1)} fusion(f32[16,128,1]{1,2,0:T(1,128)S(1)} %bitcast.574, f32[16,1,128,128]{3,2,1,0:T(8,128)S(1)} %subtract_divide_fusion.1), kind=kOutput, calls=%fused_computation.104 | convolution fusion | flops 3145728 | bytes 1064960 | tf_op jit(solution)/shard_map/bhij,bhj->bhi/dot_general | solution.py:16
  88.5 2.0 %subtract_divide_fusion = f32[16,1,128,128]{3,2,1,0:T(8,128)S(1)} fusion(f32[16]{0:T(128)S(1)} %get-tuple-element.63, f32[16,128]{1,0:T(8,128)S(1)} %bitcast.555, f32[16]{0:T(128)S(1)} %get-tuple-element.64, f32[16]{0:T(128)S(1)} %get-tuple-element.62, f32[16]{0:T(128)S(1)} %get-tuple-element.61, f32[16,128]{1,0:T(8,128)S(1)} %bitcast.546, ...), kind=kLoop, calls=%fused_computation.143 | loop fusion | flops 5242880 | bytes 2138752 | tf_op jit(solution)/shard_map/div | solution.py:18
  92.3 1.7 %fusion.99 = f32[16,1,128]{2,1,0:T(1,128)S(1)} fusion(f32[16,128,1]{1,2,0:T(1,128)S(1)} %bitcast.577, f32[16,1,128,128]{3,2,1,0:T(8,128)S(1)} %subtract_divide_fusion), kind=kOutput, calls=%fused_computation.99 | convolution fusion | flops 3145728 | bytes 1064960 | tf_op jit(solution)/shard_map/bhij,bhj->bhi/dot_general | solution.py:16
  94.2 1.7 %fusion.117 = f32[16,1,128]{2,1,0:T(1,128)S(1)} fusion(f32[16,128,1]{1,2,0:T(1,128)S(1)} %convolution_bitcast_fusion.4, f32[16,1,128,128]{3,2,1,0:T(8,128)S(1)} %get-tuple-element.53), kind=kOutput, calls=%fused_computation.117 | convolution fusion | flops 3145728 | bytes 1064960 | tf_op jit(solution)/shard_map/bhij,bhj->bhi/dot_general | solution.py:23
  95.9 1.9 %fusion.112 = f32[16,1,128]{2,1,0:T(1,128)S(1)} fusion(f32[16,128,1]{1,2,0:T(1,128)S(1)} %convolution_bitcast_fusion.3, f32[16,1,128,128]{3,2,1,0:T(8,128)S(1)} %get-tuple-element.53, f32[16,128]{1,0:T(8,128)S(1)} %bitcast.557, f32[16,128]{1,0:T(8,128)S(1)} %get-tuple-element.38, f32[16]{0:T(128)S(1)} %get-tuple-element.60), kind=kOutput, calls=%fused_computation.112 | convolution fusion | flops 3932160 | bytes 1081408 | tf_op jit(solution)/shard_map/bhij,bhj->bhi/dot_general | solution.py:23
  97.8 2.1 %fusion.107 = f32[16,1,128]{2,1,0:T(1,128)S(1)} fusion(f32[16,128,1]{1,2,0:T(1,128)S(1)} %convolution_bitcast_fusion.2, f32[16,1,128,128]{3,2,1,0:T(8,128)S(1)} %get-tuple-element.53, f32[16,128]{1,0:T(8,128)S(1)} %bitcast.571, f32[16,128]{1,0:T(8,128)S(1)} %get-tuple-element.35, f32[16]{0:T(128)S(1)} %get-tuple-element.62, f32[16,128]{1,0:T(8,128)S(1)} %bitcast.558, ...), kind=kOutput, calls=%fused_computation.107 | convolution fusion | flops 4718592 | bytes 1097856 | tf_op jit(solution)/shard_map/bhij,bhj->bhi/dot_general | solution.py:23
  99.9 2.8 %fusion.102 = f32[16,1,128]{2,1,0:T(1,128)S(1)} fusion(f32[16,128,1]{1,2,0:T(1,128)S(1)} %convolution_bitcast_fusion.1, f32[16,128]{1,0:T(8,128)S(1)} %bitcast.575, f32[16,128]{1,0:T(8,128)S(1)} %get-tuple-element.32, f32[16]{0:T(128)S(1)} %get-tuple-element.64, f32[16,1,128,128]{3,2,1,0:T(8,128)S(1)} %get-tuple-element.53, f32[16,128]{1,0:T(8,128)S(1)} %bitcast.572, ...), kind=kOutput, calls=%fused_computation.102 | convolution fusion | flops 5505024 | bytes 1114304 | tf_op jit(solution)/shard_map/bhij,bhj->bhi/dot_general | solution.py:23
  102.9 1.9 %convolution_bitcast_fusion = f32[16,128,1]{1,2,0:T(1,128)S(1)} fusion(f32[16,128,1]{1,2,0:T(1,128)S(1)} %bitcast.591, f32[16,1,128,128]{3,2,1,0:T(8,128)S(1)} %subtract_divide_fusion, f32[16]{0:T(128)S(1)} %get-tuple-element.65, f32[16,128]{1,0:T(8,128)S(1)} %bitcast.588, f32[16]{0:T(128)S(1)} %get-tuple-element.66), kind=kOutput, calls=%fused_computation.24 | convolution fusion | flops 4194304 | bytes 1073280 | tf_op jit(solution)/shard_map/bhij,bhj->bhi/dot_general | solution.py:22
  104.8 3.3 %fusion.97 = f32[16,1,128]{2,1,0:T(1,128)S(1)} fusion(f32[16,128,1]{1,2,0:T(1,128)S(1)} %convolution_bitcast_fusion, f32[16,128]{1,0:T(8,128)S(1)} %bitcast.578, f32[16,128]{1,0:T(8,128)S(1)} %get-tuple-element.29, f32[16]{0:T(128)S(1)} %get-tuple-element.66, f32[16,128]{1,0:T(8,128)S(1)} %bitcast.576, f32[16,128]{1,0:T(8,128)S(1)} %get-tuple-element.32, ...), kind=kOutput, calls=%fused_computation.97 | convolution fusion | flops 6291456 | bytes 1130752 | tf_op jit(solution)/shard_map/bhij,bhj->bhi/dot_general | solution.py:23
  108.2 11.6 %psum.7 = f32[8,16]{1,0:T(8,128)S(1)} all-reduce(f32[8,16]{1,0:T(8,128)S(1)} %multiply_reduce_fusion), channel_id=1, replica_groups=mesh['batch'=8,'head'=4] {'head'}, use_global_device_ids=true, to_apply=%region_25.26 | all-reduce | flops 128 | bytes 1024 | tf_op jit(solution)/shard_map/psum | solution.py:51
  121.2 25.6 %reduce-scatter.2.cloned.1.call-done = f32[8,16,512]{2,1,0:T(8,128)} async-done(((f32[8,16,2048]{2,1,0:T(8,128)}), f32[8,16,512]{2,1,0:T(8,128)}) %reduce-scatter.2.cloned.1.call-update) | async-done | bytes 262160 | tf_op jit(solution)/shard_map/reduce_scatter | solution.py:59
  (176 shorter events, 56.8 us)
Async XLA Ops:
  6.5 140.3 %reduce-scatter.2.cloned.1.call-start = ((), (), s32[]{:S(2)}) async-start(), calls=%async_computation.1 | async-start | bytes 1310720 | tf_op jit(solution)/shard_map/reduce_scatter | solution.py:59
  7.5 14.6 %collective-permute-start.3 = (bf16[16,512]{1,0:T(8,128)(2,1)S(1)}, bf16[16,512]{1,0:T(8,128)(2,1)S(1)}, u32[]{:S(2)}, u32[]{:S(2)}) collective-permute-start(bf16[16,512]{1,0:T(8,128)(2,1)S(1)} %get-tuple-element.26), channel_id=1, source_target_pairs={{0,1},{1,2},{2,3},{3,0},{4,5},{5,6},{6,7},{7,4},{8,9},{9,10},{10,1... | collective-permute-start | bytes 49160 | tf_op jit(solution)/shard_map/ppermute | solution.py:43
  10.6 13.1 %collective-permute-start = (bf16[16,512]{1,0:T(8,128)(2,1)S(1)}, bf16[16,512]{1,0:T(8,128)(2,1)S(1)}, u32[]{:S(2)}, u32[]{:S(2)}) collective-permute-start(bf16[16,512]{1,0:T(8,128)(2,1)S(1)} %get-tuple-element.27), channel_id=1, source_target_pairs={{0,1},{1,2},{2,3},{3,0},{4,5},{5,6},{6,7},{7,4},{8,9},{9,10},{10,1... | collective-permute-start | bytes 49160 | tf_op jit(solution)/shard_map/ppermute | solution.py:43
  12.2 13.2 %collective-permute-start.9 = (bf16[16,512]{1,0:T(8,128)(2,1)S(1)}, bf16[16,512]{1,0:T(8,128)(2,1)S(1)}, u32[]{:S(2)}, u32[]{:S(2)}) collective-permute-start(bf16[16,512]{1,0:T(8,128)(2,1)S(1)} %get-tuple-element.24), channel_id=1, source_target_pairs={{0,1},{1,2},{2,3},{3,0},{4,5},{5,6},{6,7},{7,4},{8,9},{9,10},{10,1... | collective-permute-start | bytes 49160 | tf_op jit(solution)/shard_map/ppermute | solution.py:43
  13.8 11.7 %collective-permute-start.6 = (bf16[16,512]{1,0:T(8,128)(2,1)S(1)}, bf16[16,512]{1,0:T(8,128)(2,1)S(1)}, u32[]{:S(2)}, u32[]{:S(2)}) collective-permute-start(bf16[16,512]{1,0:T(8,128)(2,1)S(1)} %get-tuple-element.25), channel_id=1, source_target_pairs={{0,1},{1,2},{2,3},{3,0},{4,5},{5,6},{6,7},{7,4},{8,9},{9,10},{10,1... | collective-permute-start | bytes 49160 | tf_op jit(solution)/shard_map/ppermute | solution.py:43
  13.8 13.3 %collective-permute-start.15 = (bf16[16,512]{1,0:T(8,128)(2,1)S(1)}, bf16[16,512]{1,0:T(8,128)(2,1)S(1)}, u32[]{:S(2)}, u32[]{:S(2)}) collective-permute-start(bf16[16,512]{1,0:T(8,128)(2,1)S(1)} %get-tuple-element.22), channel_id=1, source_target_pairs={{0,1},{1,2},{2,3},{3,0},{4,5},{5,6},{6,7},{7,4},{8,9},{9,10},{10,1... | collective-permute-start | bytes 49160 | tf_op jit(solution)/shard_map/ppermute | solution.py:43
  22.1 6.6 %collective-permute-start.12 = (bf16[16,512]{1,0:T(8,128)(2,1)S(1)}, bf16[16,512]{1,0:T(8,128)(2,1)S(1)}, u32[]{:S(2)}, u32[]{:S(2)}) collective-permute-start(bf16[16,512]{1,0:T(8,128)(2,1)S(1)} %get-tuple-element.23), channel_id=1, source_target_pairs={{0,1},{1,2},{2,3},{3,0},{4,5},{5,6},{6,7},{7,4},{8,9},{9,10},{10,1... | collective-permute-start | bytes 49160 | tf_op jit(solution)/shard_map/ppermute | solution.py:43
  23.8 6.6 %collective-permute-start.21 = (bf16[16,512]{1,0:T(8,128)(2,1)S(1)}, bf16[16,512]{1,0:T(8,128)(2,1)S(1)}, u32[]{:S(2)}, u32[]{:S(2)}) collective-permute-start(bf16[16,512]{1,0:T(8,128)(2,1)S(1)} %get-tuple-element.21), channel_id=1, source_target_pairs={{0,1},{1,2},{2,3},{3,0},{4,5},{5,6},{6,7},{7,4},{8,9},{9,10},{10,1... | collective-permute-start | bytes 49160 | tf_op jit(solution)/shard_map/ppermute | solution.py:43
  25.3 5.5 %collective-permute-start.18 = (bf16[16,512]{1,0:T(8,128)(2,1)S(1)}, bf16[16,512]{1,0:T(8,128)(2,1)S(1)}, u32[]{:S(2)}, u32[]{:S(2)}) collective-permute-start(bf16[16,512]{1,0:T(8,128)(2,1)S(1)} %get-tuple-element.28), channel_id=1, source_target_pairs={{0,1},{1,2},{2,3},{3,0},{4,5},{5,6},{6,7},{7,4},{8,9},{9,10},{10,1... | collective-permute-start | bytes 49160 | tf_op jit(solution)/shard_map/ppermute | solution.py:43
  25.4 6.7 %collective-permute-start.4 = (bf16[16,512]{1,0:T(8,128)(2,1)S(1)}, bf16[16,512]{1,0:T(8,128)(2,1)S(1)}, u32[]{:S(2)}, u32[]{:S(2)}) collective-permute-start(bf16[16,512]{1,0:T(8,128)(2,1)S(1)} %collective-permute-done.3), channel_id=1, source_target_pairs={{0,1},{1,2},{2,3},{3,0},{4,5},{5,6},{6,7},{7,4},{8,9},{9,10},{10,1... | collective-permute-start | bytes 49160 | tf_op jit(solution)/shard_map/ppermute | solution.py:43
  27.1 6.6 %collective-permute-start.1 = (bf16[16,512]{1,0:T(8,128)(2,1)S(1)}, bf16[16,512]{1,0:T(8,128)(2,1)S(1)}, u32[]{:S(2)}, u32[]{:S(2)}) collective-permute-start(bf16[16,512]{1,0:T(8,128)(2,1)S(1)} %collective-permute-done), channel_id=1, source_target_pairs={{0,1},{1,2},{2,3},{3,0},{4,5},{5,6},{6,7},{7,4},{8,9},{9,10},{10,1... | collective-permute-start | bytes 49160 | tf_op jit(solution)/shard_map/ppermute | solution.py:43
  28.7 6.6 %collective-permute-start.10 = (bf16[16,512]{1,0:T(8,128)(2,1)S(1)}, bf16[16,512]{1,0:T(8,128)(2,1)S(1)}, u32[]{:S(2)}, u32[]{:S(2)}) collective-permute-start(bf16[16,512]{1,0:T(8,128)(2,1)S(1)} %collective-permute-done.9), channel_id=1, source_target_pairs={{0,1},{1,2},{2,3},{3,0},{4,5},{5,6},{6,7},{7,4},{8,9},{9,10},{10,1... | collective-permute-start | bytes 49160 | tf_op jit(solution)/shard_map/ppermute | solution.py:43
  30.3 5.5 %collective-permute-start.7 = (bf16[16,512]{1,0:T(8,128)(2,1)S(1)}, bf16[16,512]{1,0:T(8,128)(2,1)S(1)}, u32[]{:S(2)}, u32[]{:S(2)}) collective-permute-start(bf16[16,512]{1,0:T(8,128)(2,1)S(1)} %collective-permute-done.6), channel_id=1, source_target_pairs={{0,1},{1,2},{2,3},{3,0},{4,5},{5,6},{6,7},{7,4},{8,9},{9,10},{10,1... | collective-permute-start | bytes 49160 | tf_op jit(solution)/shard_map/ppermute | solution.py:43
  30.9 6.2 %collective-permute-start.16 = (bf16[16,512]{1,0:T(8,128)(2,1)S(1)}, bf16[16,512]{1,0:T(8,128)(2,1)S(1)}, u32[]{:S(2)}, u32[]{:S(2)}) collective-permute-start(bf16[16,512]{1,0:T(8,128)(2,1)S(1)} %collective-permute-done.15), channel_id=1, source_target_pairs={{0,1},{1,2},{2,3},{3,0},{4,5},{5,6},{6,7},{7,4},{8,9},{9,10},{10,1... | collective-permute-start | bytes 49160 | tf_op jit(solution)/shard_map/ppermute | solution.py:43
  32.1 6.6 %collective-permute-start.13 = (bf16[16,512]{1,0:T(8,128)(2,1)S(1)}, bf16[16,512]{1,0:T(8,128)(2,1)S(1)}, u32[]{:S(2)}, u32[]{:S(2)}) collective-permute-start(bf16[16,512]{1,0:T(8,128)(2,1)S(1)} %collective-permute-done.12), channel_id=1, source_target_pairs={{0,1},{1,2},{2,3},{3,0},{4,5},{5,6},{6,7},{7,4},{8,9},{9,10},{10,1... | collective-permute-start | bytes 49160 | tf_op jit(solution)/shard_map/ppermute | solution.py:43
  33.7 6.6 %collective-permute-start.22 = (bf16[16,512]{1,0:T(8,128)(2,1)S(1)}, bf16[16,512]{1,0:T(8,128)(2,1)S(1)}, u32[]{:S(2)}, u32[]{:S(2)}) collective-permute-start(bf16[16,512]{1,0:T(8,128)(2,1)S(1)} %collective-permute-done.21), channel_id=1, source_target_pairs={{0,1},{1,2},{2,3},{3,0},{4,5},{5,6},{6,7},{7,4},{8,9},{9,10},{10,1... | collective-permute-start | bytes 49160 | tf_op jit(solution)/shard_map/ppermute | solution.py:43
  35.9 6.2 %collective-permute-start.5 = (bf16[16,512]{1,0:T(8,128)(2,1)S(1)}, bf16[16,512]{1,0:T(8,128)(2,1)S(1)}, u32[]{:S(2)}, u32[]{:S(2)}) collective-permute-start(bf16[16,512]{1,0:T(8,128)(2,1)S(1)} %collective-permute-done.4), channel_id=1, source_target_pairs={{0,1},{1,2},{2,3},{3,0},{4,5},{5,6},{6,7},{7,4},{8,9},{9,10},{10,1... | collective-permute-start | bytes 49160 | tf_op jit(solution)/shard_map/ppermute | solution.py:43
  37.1 6.6 %collective-permute-start.2 = (bf16[16,512]{1,0:T(8,128)(2,1)S(1)}, bf16[16,512]{1,0:T(8,128)(2,1)S(1)}, u32[]{:S(2)}, u32[]{:S(2)}) collective-permute-start(bf16[16,512]{1,0:T(8,128)(2,1)S(1)} %collective-permute-done.1), channel_id=1, source_target_pairs={{0,1},{1,2},{2,3},{3,0},{4,5},{5,6},{6,7},{7,4},{8,9},{9,10},{10,1... | collective-permute-start | bytes 49160 | tf_op jit(solution)/shard_map/ppermute | solution.py:43
  38.7 9.6 %collective-permute-start.11 = (bf16[16,512]{1,0:T(8,128)(2,1)S(1)}, bf16[16,512]{1,0:T(8,128)(2,1)S(1)}, u32[]{:S(2)}, u32[]{:S(2)}) collective-permute-start(bf16[16,512]{1,0:T(8,128)(2,1)S(1)} %collective-permute-done.10), channel_id=1, source_target_pairs={{0,1},{1,2},{2,3},{3,0},{4,5},{5,6},{6,7},{7,4},{8,9},{9,10},{10,1... | collective-permute-start | bytes 49160 | tf_op jit(solution)/shard_map/ppermute | solution.py:43
  40.3 9.1 %collective-permute-start.8 = (bf16[16,512]{1,0:T(8,128)(2,1)S(1)}, bf16[16,512]{1,0:T(8,128)(2,1)S(1)}, u32[]{:S(2)}, u32[]{:S(2)}) collective-permute-start(bf16[16,512]{1,0:T(8,128)(2,1)S(1)} %collective-permute-done.7), channel_id=1, source_target_pairs={{0,1},{1,2},{2,3},{3,0},{4,5},{5,6},{6,7},{7,4},{8,9},{9,10},{10,1... | collective-permute-start | bytes 49160 | tf_op jit(solution)/shard_map/ppermute | solution.py:43
  40.8 30.4 %collective-permute-start.17 = (bf16[16,512]{1,0:T(8,128)(2,1)S(1)}, bf16[16,512]{1,0:T(8,128)(2,1)S(1)}, u32[]{:S(2)}, u32[]{:S(2)}) collective-permute-start(bf16[16,512]{1,0:T(8,128)(2,1)S(1)} %collective-permute-done.16), channel_id=1, source_target_pairs={{0,1},{1,2},{2,3},{3,0},{4,5},{5,6},{6,7},{7,4},{8,9},{9,10},{10,1... | collective-permute-start | bytes 49160 | tf_op jit(solution)/shard_map/ppermute | solution.py:43
  42.1 29.2 %collective-permute-start.14 = (bf16[16,512]{1,0:T(8,128)(2,1)S(1)}, bf16[16,512]{1,0:T(8,128)(2,1)S(1)}, u32[]{:S(2)}, u32[]{:S(2)}) collective-permute-start(bf16[16,512]{1,0:T(8,128)(2,1)S(1)} %collective-permute-done.13), channel_id=1, source_target_pairs={{0,1},{1,2},{2,3},{3,0},{4,5},{5,6},{6,7},{7,4},{8,9},{9,10},{10,1... | collective-permute-start | bytes 49160 | tf_op jit(solution)/shard_map/ppermute | solution.py:43
  43.7 38.3 %collective-permute-start.23 = (bf16[16,512]{1,0:T(8,128)(2,1)S(1)}, bf16[16,512]{1,0:T(8,128)(2,1)S(1)}, u32[]{:S(2)}, u32[]{:S(2)}) collective-permute-start(bf16[16,512]{1,0:T(8,128)(2,1)S(1)} %collective-permute-done.22), channel_id=1, source_target_pairs={{0,1},{1,2},{2,3},{3,0},{4,5},{5,6},{6,7},{7,4},{8,9},{9,10},{10,1... | collective-permute-start | bytes 49160 | tf_op jit(solution)/shard_map/ppermute | solution.py:43
  48.4 33.6 %collective-permute-start.20 = (bf16[16,512]{1,0:T(8,128)(2,1)S(1)}, bf16[16,512]{1,0:T(8,128)(2,1)S(1)}, u32[]{:S(2)}, u32[]{:S(2)}) collective-permute-start(bf16[16,512]{1,0:T(8,128)(2,1)S(1)} %collective-permute-done.19), channel_id=1, source_target_pairs={{0,1},{1,2},{2,3},{3,0},{4,5},{5,6},{6,7},{7,4},{8,9},{9,10},{10,1... | collective-permute-start | bytes 49160 | tf_op jit(solution)/shard_map/ppermute | solution.py:43
  (7 other events, 80.5 us)
Sparse Core Ops, SparseCore 0:
  121.3 25.4 reduce-scatter.1
